TPU v7x, 128 devices: a whole 4x4x4 slice. The times are simulated.
128 devices in a mesh: tasks: 1, cols: 2 (over core), rows: 64 (over z, y, x).
Axes of the slice: x: 4, y: 4, z: 4, core: 2. Of those that a mesh axis runs over, the one named last changes fastest.
Arguments:
- points: bfloat16 [131072, 128], P(('tasks', 'rows', 'cols'))
- rhs_vecs: bfloat16 [131072, 128], P(('tasks', 'rows', 'cols'))
- lengthscale: float32 [1], replicated
- outputscale: float32 [1], replicated
Outputs:
- output: float32 [131072, 128], P(('tasks', 'rows', 'cols'))
All inputs are finite; a program needn't handle non-finite values.
Results may differ from a plain program's by a relative error of at most 0.001.
Values are sent between devices in bfloat16 or wider.
A program may use at most 1 GiB of HBM per device.

v0:
```python
import jax
import jax.numpy as jnp
from jax import lax
from jax.sharding import PartitionSpec as P


def solution(mesh):
    row_spec = P(('tasks', 'rows', 'cols'), None)

    def per_device(pts_blk, vecs_blk, lengthscale, outputscale):
        two_ell_sq = 2.0 * lengthscale[0] * lengthscale[0]
        out_scale = outputscale[0]
        row_pts = lax.all_gather(pts_blk, 'cols', axis=0, tiled=True)
        col_pts = lax.all_gather(pts_blk, 'rows', axis=0)
        col_vecs = lax.all_gather(vecs_blk, 'rows', axis=0)
        row_norms = jnp.sum(jnp.square(row_pts.astype(jnp.float32)), axis=1)
        col_norms = jnp.sum(jnp.square(col_pts.astype(jnp.float32)), axis=2)

        def col_step(run_sum, col_blk):
            blk_pts, blk_vecs, blk_norms = col_blk
            gram_mat = jnp.einsum('id,jd->ij', row_pts, blk_pts, preferred_element_type=jnp.float32)
            sq_dist = jnp.maximum(row_norms[:, None] + blk_norms[None, :] - 2.0 * gram_mat, 0.0)
            kern_blk = (out_scale * jnp.exp(-sq_dist / two_ell_sq)).astype(jnp.bfloat16)
            return run_sum + jnp.dot(kern_blk, blk_vecs, preferred_element_type=jnp.float32), None

        zero_acc = jnp.zeros((row_pts.shape[0], vecs_blk.shape[1]), jnp.float32)
        partial_rows, _ = lax.scan(col_step, zero_acc, (col_pts, col_vecs, col_norms))
        return lax.psum_scatter(partial_rows, 'cols', scatter_dimension=0, tiled=True)

    return jax.shard_map(per_device, mesh=mesh, in_specs=(row_spec, row_spec, P(None), P(None)), out_specs=row_spec, check_vma=False)
```

profile of v0, /device:TPU:1, one launch (start us, length us, event | category | flops | bytes accessed | tf_op | source)
XLA Modules:
  0.0 598.5 jit_solution(5432481640116212197)
XLA Ops:
  12.2 104.9 %all-gather.5.cloned.1.call-done = bf16[65536,128]{1,0:T(8,128)(2,1)} async-done(((bf16[1024,128]{1,0:T(8,128)(2,1)}), bf16[65536,128]{1,0:T(8,128)(2,1)}) %all-gather.5.cloned.1.call-update) | async-done | bytes 16777232 | tf_op jit(solution)/shard_map/all_gather | solution.py:14
  117.1 12.5 %multiply_reduce_fusion = f32[64,1024]{1,0:T(8,128)S(1)} fusion(bf16[64,1024,128]{2,1,0:T(8,128)(2,1)} %bitcast.41), kind=kLoop, calls=%fused_computation.16 | loop fusion | flops 25100288 | bytes 17039360 | tf_op jit(solution)/shard_map/reduce_sum | solution.py:17
  129.6 93.9 %all-gather.7.cloned.1.call-done = bf16[65536,128]{1,0:T(8,128)(2,1)} async-done(((bf16[1024,128]{1,0:T(8,128)(2,1)}), bf16[65536,128]{1,0:T(8,128)(2,1)}) %all-gather.7.cloned.1.call-update) | async-done | bytes 16777232 | tf_op jit(solution)/shard_map/all_gather | solution.py:15
  223.6 355.9 %while.11 = (s32[]{:T(128)}, f32[2048,128]{1,0:T(8,128)S(1)}, f32[]{:T(128)}, f32[2048]{0:T(1024)S(1)}, f32[64,1024]{1,0:T(8,128)S(1)}, /*index=5*/bf16[64,1024,...) while((s32[]{:T(128)}, f32[2048,128]{1,0:T(8,128)S(1)}, ...), condition=%wide.region_3.4_spmd.clone, body=%wide.region_2.3_spmd.clone.sunk | while | flops 1091043328 | bytes 3168379 | solution.py:27
  229.1 5.5 convolution_add_fusion.2
  234.7 5.5 convolution_add_fusion.2
  240.2 5.5 convolution_add_fusion.2
  245.8 5.5 convolution_add_fusion.2
  251.4 5.5 convolution_add_fusion.2
  256.9 5.5 convolution_add_fusion.2
  262.5 5.5 convolution_add_fusion.2
  268.1 5.5 convolution_add_fusion.2
  273.6 5.5 convolution_add_fusion.2
  279.2 5.5 convolution_add_fusion.2
  284.7 5.5 convolution_add_fusion.2
  290.3 5.5 convolution_add_fusion.2
  295.9 5.5 convolution_add_fusion.2
  301.4 5.5 convolution_add_fusion.2
  307.0 5.5 convolution_add_fusion.2
  312.6 5.5 convolution_add_fusion.2
  318.1 5.5 convolution_add_fusion.2
  323.7 5.5 convolution_add_fusion.2
  329.2 5.5 convolution_add_fusion.2
  334.8 5.5 convolution_add_fusion.2
  340.4 5.5 convolution_add_fusion.2
  345.9 5.5 convolution_add_fusion.2
  351.5 5.5 convolution_add_fusion.2
  357.1 5.5 convolution_add_fusion.2
  362.6 5.5 convolution_add_fusion.2
  368.2 5.5 convolution_add_fusion.2
  373.7 5.5 convolution_add_fusion.2
  379.3 5.5 convolution_add_fusion.2
  384.9 5.5 convolution_add_fusion.2
  390.4 5.5 convolution_add_fusion.2
  396.0 5.5 convolution_add_fusion.2
  401.5 5.5 convolution_add_fusion.2
  407.1 5.5 convolution_add_fusion.2
  412.7 5.5 convolution_add_fusion.2
  418.2 5.5 convolution_add_fusion.2
  423.8 5.5 convolution_add_fusion.2
  429.4 5.5 convolution_add_fusion.2
  434.9 5.5 convolution_add_fusion.2
  440.5 5.5 convolution_add_fusion.2
  446.0 5.5 convolution_add_fusion.2
  451.6 5.5 convolution_add_fusion.2
  457.2 5.5 convolution_add_fusion.2
  462.7 5.5 convolution_add_fusion.2
  468.3 5.5 convolution_add_fusion.2
  473.9 5.5 convolution_add_fusion.2
  479.4 5.5 convolution_add_fusion.2
  485.0 5.5 convolution_add_fusion.2
  490.5 5.5 convolution_add_fusion.2
  501.7 5.5 convolution_add_fusion.2
  507.2 5.5 convolution_add_fusion.2
  512.8 5.5 convolution_add_fusion.2
  523.9 5.5 convolution_add_fusion.2
  529.5 5.5 convolution_add_fusion.2
  535.0 5.5 convolution_add_fusion.2
  546.2 5.5 convolution_add_fusion.2
  551.7 5.5 convolution_add_fusion.2
  557.3 5.5 convolution_add_fusion.2
  568.4 5.5 convolution_add_fusion.2
  574.0 5.5 convolution_add_fusion.2
  580.5 11.5 %reduce-scatter.2.cloned.1.call-done = f32[1024,128]{1,0:T(8,128)} async-done(((f32[2048,128]{1,0:T(8,128)}), f32[1024,128]{1,0:T(8,128)}) %reduce-scatter.2.cloned.1.call-update) | async-done | bytes 524304 | tf_op jit(solution)/shard_map/reduce_scatter | solution.py:28
  (80 shorter events, 34.3 us)
Async XLA Ops:
  6.5 110.6 %all-gather.5.cloned.1.call-start = ((), (), s32[]{:S(2)}) async-start(), calls=%async_computation.2 | async-start | bytes 17039360 | tf_op jit(solution)/shard_map/all_gather | solution.py:14
  7.3 216.3 %all-gather.7.cloned.1.call-start = ((), (), s32[]{:S(2)}) async-start(), calls=%async_computation.3 | async-start | bytes 17039360 | tf_op jit(solution)/shard_map/all_gather | solution.py:15
  8.0 584.0 %reduce-scatter.2.cloned.1.call-start = ((), (), s32[]{:S(2)}) async-start(), calls=%async_computation.1 | async-start | bytes 1572864 | tf_op jit(solution)/shard_map/reduce_scatter | solution.py:28
  579.5 1.0 copy-start
Sparse Core Ops, SparseCore 0:
  10.2 106.8 all-gather.4
  120.0 103.4 all-gather.6
  580.6 11.3 reduce-scatter.1
where the time goes:
time: 601 us; the launch traced here: 599 us
  matrix products  353 us (59%)
  waiting for transfers between devices  212 us (35%)
  between operations  13.8 us (2%)
  other arithmetic  12.8 us (2%)
    dot_general x64, matrix products, col_step(): jnp.dot(kern_blk, blk_vecs, preferred_element_type=jnp.float32)  353 us
    all_gather x1, waiting for transfers between devices, per_device(): col_pts = lax.all_gather(pts_blk, 'rows', axis=0)  105 us
    all_gather x1, waiting for transfers between devices, per_device(): col_vecs = lax.all_gather(vecs_blk, 'rows', axis=0)  93.9 us
    reduce_sum x1, other arithmetic, per_device(): col_norms = jnp.sum(jnp.square(col_pts.astype(jnp.float32)), axis=2)  12.5 us
  transfers between devices with their start and end apart: 3, of which 3 were waited for; matrix products, arithmetic and copies ran while one was open for 2% of the time, Pallas kernels for 0%

commit v1 on v0

v1 whole, which is shorter than its diff:
```python
import functools

import jax
import jax.numpy as jnp
from jax import lax
from jax.experimental import pallas as pl
from jax.experimental.pallas import tpu as pltpu
from jax.sharding import Mesh, PartitionSpec as P

F32 = jnp.float32
BF16 = jnp.bfloat16
BLK = 1024
TILE = 256
BF16_MAX = 3.3895313892515355e38


def split3(n):
    hi = lax.reduce_precision(jnp.minimum(n, BF16_MAX), 8, 7)
    r = n - hi
    mid = lax.reduce_precision(r, 8, 7)
    return hi.astype(BF16), mid.astype(BF16), (r - mid).astype(BF16)


def kernel(nblk, npair, scal_ref, xr_ref, xc_ref, ag_ref, vt_ref, yt_ref):
    negc, logs = scal_ref[0], scal_ref[1]
    cap = jnp.full((TILE, TILE), scal_ref[2], F32).astype(BF16)
    nunit = nblk * npair * 4

    def body(*accs):
        g = (accs[0:2], accs[2:4])
        y = (accs[4:6], accs[6:8])
        for ref in accs:
            pltpu.matmul_pop(ref)
        yt_ref[...] = jnp.zeros_like(yt_ref)

        def where(unit):
            step = unit // 4
            return step // npair, lax.rem(step, npair), lax.rem(unit, 4)

        def gram(unit, par):
            unit = lax.rem(unit, nunit)
            blk, pair, t = where(unit)
            rows = pl.ds(pl.multiple_of(t * TILE, TILE), TILE)
            lhs = jnp.concatenate([xc_ref[blk, rows, :], ag_ref[blk, rows, :]], axis=1)
            for q in range(2):
                cols = pl.ds(pl.multiple_of(pair * (2 * TILE) + q * TILE, TILE), TILE)
                pltpu.matmul_push_rhs(xr_ref[:, cols], 0, q)
                pltpu.matmul_acc_lhs(g[par][q], lhs, load_staged_rhs=0)

        def kern(par, q):
            d = pltpu.matmul_pop(g[par][q])
            k = jnp.exp2(d * negc + logs).astype(BF16)
            return jnp.minimum(k, cap)

        def apply(unit, ks, yp):
            blk, _, t = where(unit)
            lhs = vt_ref[blk, :, pl.ds(pl.multiple_of(t * TILE, TILE), TILE)]
            for q in range(2):
                pltpu.matmul_push_rhs(ks[q], 1, q)
                pltpu.matmul_acc_lhs(y[yp][q], lhs, load_staged_rhs=1)

        def flush(step, yp):
            step = jnp.maximum(step, 0)
            pair = lax.rem(step, npair)
            for q in range(2):
                cols = pl.ds(pl.multiple_of(pair * (2 * TILE) + q * TILE, TILE), TILE)
                yt_ref[:, cols] += pltpu.matmul_pop(y[yp][q])

        gram(0, 0)
        gram(1, 1)

        def trip(i, _):
            for u in range(8):
                unit = i * 8 + u
                ks = [kern(u % 2, q) for q in range(2)]
                gram(unit + 2, u % 2)
                apply(unit, ks, u // 4)
                if u == 2:
                    flush(i * 2 - 1, 1)
                if u == 6:
                    flush(i * 2, 0)
            return 0

        lax.fori_loop(0, nunit // 8, trip, 0)
        flush(nunit // 4 - 1, 1)
        for ref in accs:
            pltpu.matmul_pop(ref)

    acc = lambda q, m: pltpu.ACC(q)((m, TILE), F32)
    pl.run_scoped(body, acc(0, TILE), acc(1, TILE), acc(0, TILE), acc(1, TILE),
                  acc(0, 128), acc(1, 128), acc(0, 128), acc(1, 128))


def solution(mesh):
    grid = Mesh(mesh.devices.reshape(2, 4, 4, 4), ('c', 'z', 'y', 'x'))
    spec = P(('z', 'y', 'x', 'c'), None)

    def per_device(x, v, ell, scale):
        two_ell_sq = 2.0 * ell[0] * ell[0]
        s = scale[0]
        shrink = jnp.where(two_ell_sq > 1.0, 2.0 ** -6, 1.0).astype(F32)
        negc = -(1.4426950408889634 / shrink) / two_ell_sq
        scal = jnp.stack([negc, jnp.log2(jnp.abs(s)), jnp.abs(s)])

        norm = jnp.sum(jnp.square(x.astype(F32)), axis=1)
        pieces = jnp.stack(split3(norm) + (jnp.ones_like(norm, BF16),) * 3)
        aug = jnp.pad(pieces.T, ((0, 0), (0, 122)))
        rowpc = jnp.concatenate([pieces[3:], pieces[:3]], axis=0).astype(F32)
        sb = shrink
        xt = x.T.astype(F32)
        stat = jnp.concatenate([xt * (-2.0 * sb), rowpc * sb, jnp.zeros((122, BLK), F32)], axis=0).astype(BF16)

        xr = lax.all_gather(stat, 'x', axis=1, tiled=True)
        xc = lax.all_gather(x, ('z', 'y', 'c'), axis=0)
        ag = lax.all_gather(aug, ('z', 'y', 'c'), axis=0)
        vt = lax.all_gather(v.T, ('z', 'y', 'c'), axis=0)
        nblk = xc.shape[0]
        npair = xr.shape[1] // (2 * TILE)
        vm = pl.BlockSpec(memory_space=pltpu.VMEM)
        yt = pl.pallas_call(
            functools.partial(kernel, nblk, npair),
            out_shape=jax.ShapeDtypeStruct((128, xr.shape[1]), F32),
            in_specs=[pl.BlockSpec(memory_space=pltpu.SMEM), vm, vm, vm, vm],
            out_specs=vm,
            compiler_params=pltpu.CompilerParams(vmem_limit_bytes=60 * 2 ** 20),
        )(scal, xr, xc, ag, vt)
        part = yt.T * jnp.where(s < 0, -1.0, 1.0)
        return lax.psum_scatter(part, 'x', scatter_dimension=0, tiled=True)

    return jax.shard_map(per_device, mesh=grid, in_specs=(spec, spec, P(None), P(None)), out_specs=spec, check_vma=False)
```

time: 601 us -> 437 us (0.73)
  matrix products: 353 us -> 0 us
  Pallas kernels: 0 us -> 184 us
  local copies, waits for them, and re-layouts: 1.67 us -> 27.7 us
  other arithmetic: 12.8 us -> 4.87 us
  waiting for transfers between devices: 212 us -> 205 us
    dot_general x64 -> x0, matrix products: 353 us -> none  [col_step(): jnp.dot(kern_blk, blk_vecs, preferred_element_type=jnp.float32)]
    pallas_call x0 -> x1, Pallas kernels: none -> 184 us  [per_device(): pl.pallas_call(functools.partial(kernel, nblk, npair), out_shape=jax.Shap...]
    all_gather x0 -> x2, local copies, waits for them, and re-layouts: none -> 23.7 us  [the longest x1 12 us: per_device(): vt = lax.all_gather(v.T, ('z', 'y', 'c'), axis=0)]
    all_gather x2 -> x4, waiting for transfers between devices: 199 us -> 176 us  [the longest x1 55.5 us: per_device(): xc = lax.all_gather(x, ('z', 'y', 'c'), axis=0)]
    reduce_scatter x1, waiting for transfers between devices: 11.5 us -> 28.5 us  [per_device(): return lax.psum_scatter(part, 'x', scatter_dimension=0, tiled=True)]
    reduce_sum x2 -> x0, other arithmetic: 12.8 us -> none  [the longest x1 12.5 us: per_device(): col_norms = jnp.sum(jnp.square(col_pts.astype(jnp.float32)), axis=2)]
  transfers between devices with their start and end apart: 3 -> 5, of which waited for: 3 -> 5; matrix products, arithmetic and copies ran while one was open for 2% -> 6% of each run, Pallas kernels for 0% -> 0%
where the time goes in v1:
time: 437 us; the launch traced here: 436 us
  waiting for transfers between devices  205 us (47%)
  Pallas kernels  184 us (42%)
  local copies, waits for them, and re-layouts  27.7 us (6%)
  between operations  14.6 us (3%)
  other arithmetic  4.87 us (1%)
    pallas_call x1, Pallas kernels, per_device(): pl.pallas_call(functools.partial(kernel, nblk, npair), out_shape=jax.Shap...  184 us
    all_gather x1, waiting for transfers between devices, per_device(): xc = lax.all_gather(x, ('z', 'y', 'c'), axis=0)  55.5 us
    all_gather x1, waiting for transfers between devices, per_device(): ag = lax.all_gather(aug, ('z', 'y', 'c'), axis=0)  52.7 us
    all_gather x1, waiting for transfers between devices, per_device(): vt = lax.all_gather(v.T, ('z', 'y', 'c'), axis=0)  48.2 us
    reduce_scatter x1, waiting for transfers between devices, per_device(): return lax.psum_scatter(part, 'x', scatter_dimension=0, tiled=True)  28.5 us
    all_gather x1, waiting for transfers between devices, per_device(): xr = lax.all_gather(stat, 'x', axis=1, tiled=True)  19.1 us
    all_gather x1, local copies, waits for them, and re-layouts, per_device(): vt = lax.all_gather(v.T, ('z', 'y', 'c'), axis=0)  12 us
    all_gather x1, local copies, waits for them, and re-layouts, per_device(): ag = lax.all_gather(aug, ('z', 'y', 'c'), axis=0)  11.7 us
  transfers between devices with their start and end apart: 5, of which 5 were waited for; matrix products, arithmetic and copies ran while one was open for 6% of the time, Pallas kernels for 0%

profile of v1, /device:TPU:1, one launch (start us, length us, event | category | flops | bytes accessed | tf_op | source)
XLA Modules:
  0.0 436.2 jit_solution(11648952528476623729)
XLA Ops:
  6.5 0.0 all-gather.12.cloned.1.call-start
  7.2 1.1 copy.12
  8.3 0.1 fusion.2
  8.5 0.8 pad.5
  9.2 0.0 all-gather.12.cloned.1.call-update
  9.3 0.0 all-gather.14.cloned.1.call-start
  9.3 0.7 all-gather.14.cloned.1.call-update
  10.0 0.0 all-gather.8.cloned.1.call-start
  10.1 0.1 pad.8.clone
  10.2 0.9 maximum_maximum_fusion
  11.1 0.0 all-gather.8.cloned.1.call-update
  11.1 0.0 all-gather.10.cloned.1.call-start
  11.2 0.5 all-gather.10.cloned.1.call-update
  11.7 0.0 reduce-scatter.2.cloned.1.call-start
  12.5 0.7 pad_maximum_fusion.scal_ref
  13.2 52.7 %all-gather.12.cloned.1.call-done = bf16[32768,128]{0,1:T(8,128)(2,1)} async-done(((bf16[1024,128]{0,1:T(8,128)(2,1)}), bf16[32768,128]{0,1:T(8,128)(2,1)}) %all-gather.12.cloned.1.call-update) | async-done | bytes 8388624 | tf_op jit(solution)/shard_map/all_gather | solution.py:115
  65.9 11.7 %copy.13 = bf16[32768,128]{1,0:T(8,128)(2,1)} copy(bf16[32768,128]{0,1:T(8,128)(2,1)} %all-gather.12.cloned.1.call-done) | data formatting | bytes 16777216 | tf_op jit(solution)/shard_map/all_gather | solution.py:115
  77.6 48.2 %all-gather.14.cloned.1.call-done = bf16[4096,1024]{0,1:T(8,128)(2,1)} async-done(((bf16[128,1024]{0,1:T(8,128)(2,1)}), bf16[4096,1024]{0,1:T(8,128)(2,1)}) %all-gather.14.cloned.1.call-update) | async-done | bytes 8388624 | tf_op jit(solution)/shard_map/all_gather | solution.py:116
  125.8 12.0 %copy.14 = bf16[4096,1024]{1,0:T(8,128)(2,1)} copy(bf16[4096,1024]{0,1:T(8,128)(2,1)} %all-gather.14.cloned.1.call-done) | data formatting | bytes 16777216 | tf_op jit(solution)/shard_map/all_gather | solution.py:116
  137.8 19.1 %all-gather.8.cloned.1.call-done.xr_ref = bf16[256,4096]{1,0:T(8,128)(2,1)} async-done(((bf16[256,1024]{1,0:T(8,128)(2,1)}), bf16[256,4096]{1,0:T(8,128)(2,1)}) %all-gather.8.cloned.1.call-update) | async-done | bytes 2097168 | tf_op jit(solution)/shard_map/all_gather | solution.py:113
  156.9 55.5 %all-gather.10.cloned.1.call-done = bf16[32768,128]{1,0:T(8,128)(2,1)} async-done(((bf16[1024,128]{1,0:T(8,128)(2,1)}), bf16[32768,128]{1,0:T(8,128)(2,1)}) %all-gather.10.cloned.1.call-update) | async-done | bytes 8388624 | tf_op jit(solution)/shard_map/all_gather | solution.py:114
  212.4 183.6 %shard_map.46 = f32[128,4096]{1,0:T(8,128)} custom-call(f32[3]{0:T(128)} %pad_maximum_fusion.scal_ref, bf16[256,4096]{1,0:T(8,128)(2,1)} %all-gather.8.cloned.1.call-done.xr_ref, bf16[32,1024,128]{2,1,0:T(8,128)(2,1)} %bitcast.17, bf16[32,1024,128]{2,1,0:T(8,128)(2,1)} %bitcast.15, bf16[32,128,1024]{2,1,0:T(8,128)(2,1)} %bitcast.16), custom_call_target="tpu_custom_call" | custom-call | tf_op jit(solution)/shard_map/pallas_call | solution.py:120
  396.0 3.2 multiply_bitcast_fusion
  399.1 0.0 reduce-scatter.2.cloned.1.call-update
  399.2 28.5 %reduce-scatter.2.cloned.1.call-done = f32[1024,128]{0,1:T(8,128)} async-done(((f32[4096,128]{0,1:T(8,128)}), f32[1024,128]{0,1:T(8,128)}) %reduce-scatter.2.cloned.1.call-update) | async-done | bytes 524304 | tf_op jit(solution)/shard_map/reduce_scatter | solution.py:128
  427.7 2.0 copy.15
  (6 shorter events, 0.1 us)
Async XLA Ops:
  6.5 59.4 %all-gather.12.cloned.1.call-start = ((), (), s32[]{:S(2)}) async-start(), calls=%async_computation.4 | async-start | bytes 8650752 | tf_op jit(solution)/shard_map/all_gather | solution.py:115
  9.3 116.6 %all-gather.14.cloned.1.call-start = ((), (), s32[]{:S(2)}) async-start(), calls=%async_computation.5 | async-start | bytes 8650752 | tf_op jit(solution)/shard_map/all_gather | solution.py:116
  10.0 146.9 %all-gather.8.cloned.1.call-start = ((), (), s32[]{:S(2)}) async-start(), calls=%async_computation.1 | async-start | bytes 2621440 | tf_op jit(solution)/shard_map/all_gather | solution.py:113
  11.1 201.3 %all-gather.10.cloned.1.call-start = ((), (), s32[]{:S(2)}) async-start(), calls=%async_computation.3 | async-start | bytes 8650752 | tf_op jit(solution)/shard_map/all_gather | solution.py:114
  11.7 415.9 %reduce-scatter.2.cloned.1.call-start = ((), (), s32[]{:S(2)}) async-start(), calls=%async_computation.2 | async-start | bytes 2621440 | tf_op jit(solution)/shard_map/reduce_scatter | solution.py:128
Sparse Core Ops, SparseCore 0:
  9.6 56.2 all-gather.11
  68.1 57.7 all-gather.13
  127.5 29.3 all-gather.7
  159.1 53.2 all-gather.9
  399.3 28.3 reduce-scatter.1

commit v2 on v0

v2 whole, which is shorter than its diff:
```python
import functools

import jax
import jax.numpy as jnp
from jax import lax
from jax.experimental import pallas as pl
from jax.experimental.pallas import tpu as pltpu
from jax.sharding import Mesh, PartitionSpec as P

F32 = jnp.float32
BF16 = jnp.bfloat16
MESH = pl.DeviceIdType.MESH
BLK = 1024
TILE = 256
HALF = 512
AUG0 = 2 * HALF
ROWS = AUG0 + 4 * 8
XROWS = 144
BF16_MAX = 3.3895313892515355e38

A, B = 0, 1
ORDER = [(0, 0, A), (0, 0, B),
         (0, -1, A), (0, 1, A), (-1, 0, B), (1, 0, B),
         (0, -1, B), (0, 1, B), (-1, 0, A), (1, 0, A),
         (-1, -1, B), (-1, 1, B), (-1, -1, A), (1, -1, A),
         (1, -1, B), (1, 1, B), (-1, 1, A), (1, 1, A),
         (0, 2, A), (2, 0, B), (0, 2, B), (2, 0, A),
         (2, -1, B), (2, 1, B), (-1, 2, A), (1, 2, A),
         (-1, 2, B), (1, 2, B), (2, -1, A), (2, 1, A),
         (2, 2, B), (2, 2, A)]
POS = {key: i for i, key in enumerate(ORDER)}
NPOS = len(ORDER)


def wrap(d):
    return (d + 1) % 4 - 1


def split3(n):
    hi = lax.reduce_precision(jnp.minimum(n, BF16_MAX), 8, 7)
    r = n - hi
    mid = lax.reduce_precision(r, 8, 7)
    return hi.astype(BF16), mid.astype(BF16), (r - mid).astype(BF16)


class Wires:
    def __init__(self, cols, send, ici, d2d, pos):
        self.cols, self.send, self.ici, self.d2d, self.pos = cols, send, ici, d2d, pos
        self.sent = []
        self.dev = {(a, d): {a: lax.rem(pos[a] + d + 4, 4)} for a in 'zyx' for d in (1, -1, 2)}
        self.mate = {'c': 1 - pos['c']}

    def _copy(self, src, dst, recv, dev):
        n = len(self.sent)
        self.sent.append(lambda: pltpu.make_async_copy(src(), src(), self.send.at[n]).wait())
        pltpu.make_async_remote_copy(src_ref=src(), dst_ref=dst(), send_sem=self.send.at[n], recv_sem=recv(),
                                     device_id=dev, device_id_type=MESH).start()

    def block(self, key, c=0, part=None):
        p = POS[key]
        if part is None:
            return lambda: self.cols.at[p, c]
        return lambda: self.cols.at[p, c, pl.ds(part * (ROWS // 2), ROWS // 2)]

    def sem(self, key, part=0):
        return lambda: self.ici.at[POS[key], part]

    def both(self, axis, key):
        for sign in (1, -1):
            dz, dy, h = key
            dst = (dz, wrap(dy - sign), h) if axis == 'y' else (wrap(dz - sign), dy, h)
            self._copy(self.block(key), self.block(dst), self.sem(dst), self.dev[axis, sign])

    def relay(self, axis, off, h):
        dst = (off, 2, h) if axis == 'y' else (2, off, h)
        for part, sign in ((0, 1), (1, -1)):
            src = (off, -sign, h) if axis == 'y' else (-sign, off, h)
            self._copy(self.block(src, 0, part), self.block(dst, 0, part), self.sem(dst, part), self.dev[axis, sign])

    def partner(self, key):
        self._copy(self.block(key, 0), self.block(key, 1), lambda: self.d2d.at[POS[key]], self.mate)

    def _recv(self, dst, sem):
        pltpu.make_async_copy(dst, dst, sem).wait()

    def got(self, key):
        for part in (0, 1) if self.halved(key) else (None,):
            self._recv(self.block(key, 0, part)(), self.sem(key, part or 0)())

    @staticmethod
    def halved(key):
        dz, dy, h = key
        last = (dz if dz != 0 else dy) if h == A else (dy if dy != 0 else dz)
        return last == 2

    def got_partner(self, p):
        self._recv(self.cols.at[p, 1], self.d2d.at[p])


def schedule(w):
    def slot1():
        for key in [(0, -1, A), (0, 1, A), (-1, 0, B), (1, 0, B)]:
            w.got(key)
            w.partner(key)
        for d in (-1, 1):
            w.both('y', (d, 0, B))
            w.both('z', (0, d, A))
        w.relay('y', 0, A)
        w.relay('z', 0, B)

    def slot2():
        for key in [(0, -1, B), (0, 1, B), (-1, 0, A), (1, 0, A)]:
            w.got(key)
            w.partner(key)
        w.relay('y', 0, B)
        w.relay('z', 0, A)

    def slot3():
        for key in [(-1, -1, B), (-1, 1, B), (-1, -1, A), (1, -1, A)]:
            w.got(key)
            w.partner(key)

    def slot4():
        for key in [(0, 2, A), (2, 0, B)]:
            w.got(key)
            w.partner(key)
        w.both('y', (2, 0, B))
        w.both('z', (0, 2, A))
        for key in [(1, -1, B), (1, 1, B), (-1, 1, A), (1, 1, A)]:
            w.got(key)
            w.partner(key)
        for d in (-1, 1):
            w.relay('y', d, B)
            w.relay('z', d, A)

    def slot5():
        for key in [(0, 2, B), (2, 0, A)]:
            w.got(key)
            w.partner(key)

    def slot6():
        for key in [(2, -1, B), (2, 1, B), (-1, 2, A), (1, 2, A)]:
            w.got(key)
            w.partner(key)
        w.relay('y', 2, B)
        w.relay('z', 2, A)

    def slot7():
        for key in [(-1, 2, B), (1, 2, B), (2, -1, A), (2, 1, A)]:
            w.got(key)
            w.partner(key)

    def slot8():
        for key in [(2, 2, B), (2, 2, A)]:
            w.got(key)
            w.partner(key)

    return {1: slot1, 5: slot2, 8: slot3, 9: slot4, 10: slot5, 12: slot6, 14: slot7, 15: slot8}


def kernel(scal_ref, own_ref, xown_ref, out_ref, cols, ag, xr, yt, yin, local, send, ici, d2d, xsem):
    pos = {k: lax.axis_index(k) for k in ('c', 'z', 'y', 'x')}
    w = Wires(cols, send, ici, d2d, pos)
    xdev = lambda d: w.dev['x', d]

    loads = [pltpu.make_async_copy(own_ref.at[h], cols.at[h, 0], local.at[h]) for h in range(2)]
    loads.append(pltpu.make_async_copy(xown_ref, xr.at[0, :, :, pl.ds(0, XROWS)], local.at[2]))
    for cp in loads:
        cp.start()
    barrier = pltpu.get_barrier_semaphore()
    peers = [w.dev[a, d] for a in 'zy' for d in (1, -1)] + [xdev(1), xdev(-1), xdev(2), w.mate]
    for dev in peers:
        pl.semaphore_signal(barrier, inc=1, device_id=dev, device_id_type=MESH)
    xr[:, :, :, pl.ds(XROWS, TILE - XROWS), :] = jnp.zeros((4, 4, 2, TILE - XROWS, 128), BF16)
    yt[...] = jnp.zeros_like(yt)
    for cp in loads:
        cp.wait()
    pl.semaphore_wait(barrier, len(peers))

    def xcopy(src, dst, tiles, recv, d):
        cut = lambda b: lambda: xr.at[b, pl.ds(*tiles), :, pl.ds(0, XROWS)]
        w._copy(cut(src), cut(dst), lambda: xsem.at[recv], xdev(d))

    def xgot(dst, tiles, recv):
        ref = xr.at[dst, pl.ds(*tiles), :, pl.ds(0, XROWS)]
        pltpu.make_async_copy(ref, ref, xsem.at[recv]).wait()

    w.partner((0, 0, A))
    w.partner((0, 0, B))
    xcopy(0, 1, (0, 4), 0, 1)
    xcopy(0, 2, (0, 4), 1, -1)
    w.both('y', (0, 0, A))
    w.both('z', (0, 0, B))
    w.both('y', (0, 0, B))
    w.both('z', (0, 0, A))

    negc, logs = scal_ref[0], scal_ref[1]

    def build(p, c, tiles):
        for lt in tiles:
            piece = cols[p, c, pl.ds(AUG0 + lt * 8, 8), :].astype(F32)
            full = jnp.concatenate([piece, jnp.zeros((120, 128), F32)], axis=0)
            ag[p, c, pl.ds(lt * 128, 128), :] = full.T.astype(BF16)

    def work(p, xb, pair):
        lhs = jnp.concatenate([jnp.concatenate([cols[p, c, pl.ds(0, HALF), :], ag[p, c]], axis=1) for c in range(2)], axis=0)
        rhs = jnp.concatenate([jnp.concatenate([xr[xb, pair * 2 + q, h] for h in range(2)], axis=1) for q in range(2)], axis=1)
        dist = jnp.dot(lhs, rhs, preferred_element_type=F32)
        kern = jnp.exp2(dist * negc + logs).astype(BF16)
        kern = jnp.minimum(kern, jnp.full(kern.shape, scal_ref[2], F32).astype(BF16))
        vt = jnp.concatenate([cols[p, c, pl.ds(HALF + 128 * k, 128), :] for c in range(2) for k in range(4)], axis=1)
        return jnp.dot(vt, kern, preferred_element_type=F32)

    def add(xb, pair, r):
        for q in range(2):
            yt[xb, pair * 2 + q] += r[:, q * TILE:(q + 1) * TILE]

    acts = schedule(w)

    def phase_a(i, _):
        p, h = lax.div(i, 2), lax.rem(i, 2)

        @pl.when(h == 0)
        def _():
            for at, act in acts.items():
                pl.when(p == at)(act)

        @pl.when(i == 1)
        def _():
            xgot(3, (0, 2), 2)
            xgot(3, (2, 2), 3)

        @pl.when((h == 1) & (p > 0))
        def _():
            w.got_partner(p + 1)

        for k in range(2):
            for pair in range(2):
                add(2 * h + k, pair, work(p, 2 * h + k, pair))
        build(p + 1, h, range(4))
        return 0

    def phase_b1(i, _):
        p = 16 + 2 * i

        @pl.when(i < 7)
        def _():
            w.got_partner(p + 2)
            w.got_partner(p + 3)

        for pair in range(2):
            add(3, pair, work(p, 3, pair) + work(p + 1, 3, pair))
        for k in range(2):
            for c in range(2):
                build(16 + lax.rem(2 * i + 2 + k, 16), c, range(4))
        return 0

    def ysend(label, d, slot):
        return lambda: pltpu.make_async_remote_copy(src_ref=yt.at[label], dst_ref=yin.at[slot], send_sem=xsem.at[4 + slot],
                                                    recv_sem=xsem.at[7 + slot], device_id=xdev(d), device_id_type=MESH)

    sends = [ysend(3, 2, 2), ysend(2, 1, 0), ysend(1, -1, 1)]

    def phase_b2(i, _):
        for n in range(3):
            pl.when(i == 8 * n + 1)(lambda n=n: sends[n]().start())
        xb, p = 2 - lax.div(i, 8), 16 + 2 * lax.rem(i, 8)
        for pair in range(2):
            add(xb, pair, work(p, xb, pair) + work(p + 1, xb, pair))
        return 0

    for p in range(2):
        w.got_partner(p)
        if p == 0:
            for c in range(2):
                build(p, c, range(4))
    xgot(1, (0, 4), 0)
    xgot(2, (0, 4), 1)
    xcopy(1, 3, (0, 2), 2, 1)
    xcopy(2, 3, (2, 2), 3, -1)
    lax.fori_loop(0, 32, phase_a, 0)
    w.got_partner(17)
    for c in range(2):
        build(17, c, range(4))
    lax.fori_loop(0, 8, phase_b1, 0)
    lax.fori_loop(0, 24, phase_b2, 0)
    for cp in sends:
        cp().wait()
    for wait in w.sent:
        wait()
    for t in range(4):
        total = (yt[0, t] + yin[0, t] + yin[1, t] + yin[2, t]) * scal_ref[3]
        out_ref[pl.ds(t * TILE, TILE), :] = total.T


def solution(mesh):
    grid = Mesh(mesh.devices.reshape(2, 4, 4, 4), ('c', 'z', 'y', 'x'))
    spec = P(('z', 'y', 'x', 'c'), None)

    def per_device(x, v, ell, scale):
        two_ell_sq = 2.0 * ell[0] * ell[0]
        s = scale[0]
        shrink = jnp.where(two_ell_sq > 1.0, 2.0 ** -6, 1.0).astype(F32)
        negc = -(1.4426950408889634 / shrink) / two_ell_sq
        scal = jnp.stack([negc, jnp.log2(jnp.abs(s)), jnp.abs(s), jnp.where(s < 0, -1.0, 1.0)])

        norm = jnp.sum(jnp.square(x.astype(F32)), axis=1)
        pieces = jnp.stack(split3(norm) + (jnp.ones_like(norm, BF16),) * 3)
        lanes = jnp.pad(pieces, ((0, 2), (0, 0))).reshape(8, 8, 128).transpose(1, 0, 2)
        vt = v.reshape(8, 128, 128).transpose(0, 2, 1)
        own = jnp.concatenate([x.reshape(2, HALF, 128), vt.reshape(2, HALF, 128), lanes.reshape(2, 32, 128)], axis=1)

        xt = x.reshape(4, 2, 128, 128).transpose(0, 1, 3, 2).astype(F32) * (-2.0 * shrink)
        rowpc = jnp.pad(jnp.concatenate([pieces[3:], pieces[:3]]).astype(F32) * shrink, ((0, 10), (0, 0)))
        rowpc = rowpc.reshape(16, 4, 2, 128).transpose(1, 2, 0, 3)
        xown = jnp.concatenate([xt, rowpc], axis=2).astype(BF16)

        anym = pl.BlockSpec(memory_space=pl.ANY)
        return pl.pallas_call(
            kernel,
            out_shape=jax.ShapeDtypeStruct((BLK, 128), F32),
            name='comm',
            in_specs=[pl.BlockSpec(memory_space=pltpu.SMEM), anym, anym],
            out_specs=pl.BlockSpec(memory_space=pltpu.VMEM),
            scratch_shapes=[
                pltpu.VMEM((NPOS, 2, ROWS, 128), BF16),
                pltpu.VMEM((NPOS, 2, HALF, 128), BF16),
                pltpu.VMEM((4, 4, 2, TILE, 128), BF16),
                pltpu.VMEM((4, 4, 128, TILE), F32),
                pltpu.VMEM((3, 4, 128, TILE), F32),
                pltpu.SemaphoreType.DMA((3,)),
                pltpu.SemaphoreType.DMA((100,)),
                pltpu.SemaphoreType.DMA((NPOS, 2)),
                pltpu.SemaphoreType.DMA((NPOS,)),
                pltpu.SemaphoreType.DMA((10,)),
            ],
            compiler_params=pltpu.CompilerParams(vmem_limit_bytes=60 * 2 ** 20, collective_id=0, has_side_effects=True),
        )(scal, own, xown)

    return jax.shard_map(per_device, mesh=grid, in_specs=(spec, spec, P(None), P(None)), out_specs=spec, check_vma=False)
```

time: 601 us -> 155 us (0.26)
  matrix products: 353 us -> 0 us
  waiting for transfers between devices: 212 us -> 0 us
  Pallas kernels: 0 us -> 147 us
  between operations: 13.8 us -> 1.57 us
  other arithmetic: 12.8 us -> 2.43 us
    dot_general x64 -> x0, matrix products: 353 us -> none  [col_step(): jnp.dot(kern_blk, blk_vecs, preferred_element_type=jnp.float32)]
    all_gather x2 -> x0, waiting for transfers between devices: 199 us -> none  [the longest x1 105 us: per_device(): col_pts = lax.all_gather(pts_blk, 'rows', axis=0)]
    pallas_call x0 -> x1, Pallas kernels: none -> 147 us  [per_device(): pl.pallas_call(kernel, out_shape=jax.ShapeDtypeStruct((BLK, 128), F32), n...]
    reduce_sum x2 -> x0, other arithmetic: 12.8 us -> none  [the longest x1 12.5 us: per_device(): col_norms = jnp.sum(jnp.square(col_pts.astype(jnp.float32)), axis=2)]
    reduce_scatter x1 -> x0, waiting for transfers between devices: 11.5 us -> none  [per_device(): lax.psum_scatter(partial_rows, 'cols', scatter_dimension=0, tiled=True)]
  transfers between devices with their start and end apart: 3 -> 0, of which waited for: 3 -> 0; matrix products, arithmetic and copies ran while one was open for 2% -> 0% of each run, Pallas kernels for 0% -> 0%
where the time goes in v2:
time: 155 us
  Pallas kernels  147 us (95%)
  local copies, waits for them, and re-layouts  3.26 us (2%)
  other arithmetic  2.43 us (2%)
  between operations  1.57 us (1%)
    pallas_call x1, Pallas kernels, per_device(): pl.pallas_call(kernel, out_shape=jax.ShapeDtypeStruct((BLK, 128), F32), n...  147 us

profile of v2, /device:TPU:1, one launch (start us, length us, event | category | flops | bytes accessed | tf_op | source)
XLA Modules:
  0.0 154.7 jit_solution(10773058814283812403)
XLA Ops:
  0.0 0.0 copy-start
  1.5 0.6 pad_maximum_fusion.2.scal_ref
  2.1 1.1 copy.6
  3.2 0.0 copy-done
  3.2 0.2 fusion.1
  3.4 0.2 copy.7
  3.8 0.7 pad_maximum_fusion.1.xown_ref
  4.6 0.8 pad_maximum_fusion.own_ref
  5.4 147.4 %comm.1 = f32[1024,128]{1,0:T(8,128)} custom-call(f32[4]{0:T(128)} %pad_maximum_fusion.2.scal_ref, bf16[2,1056,128]{2,1,0:T(8,128)(2,1)} %pad_maximum_fusion.own_ref, bf16[4,2,144,128]{3,2,1,0:T(8,128)(2,1)} %pad_maximum_fusion.1.xown_ref), custom_call_target="tpu_custom_call" | custom-call | tf_op jit(solution)/shard_map/comm/pallas_call | solution.py:319
  152.8 1.9 %copy.14 = f32[1024,128]{1,0:T(8,128)} copy(f32[1024,128]{1,0:T(8,128)} %comm.1) | data formatting | bytes 1048576
  (9 shorter events, 0.1 us)
Async XLA Ops:
  0.0 3.2 %copy-start = (bf16[1024,128]{1,0:T(8,128)(2,1)S(1)}, bf16[1024,128]{1,0:T(8,128)(2,1)}, u32[]{:S(2)}) copy-start(bf16[1024,128]{1,0:T(8,128)(2,1)} %param.4) | copy-start | bytes 786436

commit v3 on v2

--- a/solution.py
+++ b/solution.py
@@ -155,10 +155,10 @@
             w.got(key)
             w.partner(key)
 
-    return {1: slot1, 5: slot2, 8: slot3, 9: slot4, 10: slot5, 12: slot6, 14: slot7, 15: slot8}
-
-
-def kernel(scal_ref, own_ref, xown_ref, out_ref, cols, ag, xr, yt, yin, local, send, ici, d2d, xsem):
+    return {1: slot1, 4: slot2, 8: slot3, 9: slot4, 10: slot5, 12: slot6, 14: slot7, 15: slot8}
+
+
+def kernel(scal_ref, own_ref, xown_ref, out_ref, cols, ag, xr, yt, yin, local, send, ici, d2d, xsem, ysem):
     pos = {k: lax.axis_index(k) for k in ('c', 'z', 'y', 'x')}
     w = Wires(cols, send, ici, d2d, pos)
     xdev = lambda d: w.dev['x', d]
@@ -222,8 +222,7 @@
 
         @pl.when(h == 0)
         def _():
-            for at, act in acts.items():
-                pl.when(p == at)(act)
+                pl.when(p == 1)(acts[1])
 
         @pl.when(i == 1)
         def _():
@@ -240,33 +239,52 @@
         build(p + 1, h, range(4))
         return 0
 
+    def phase_a4(n, _):
+        p = n + 2
+        for at, act in acts.items():
+            if at > 1:
+                pl.when(p == at)(act)
+        w.got_partner(p + 1)
+        late = p + lax.div(p, 12) * (5 - 3 * lax.div(p, 15))
+        pl.when((p >= 12) & (p < 15))(lambda: w.got_partner(p + 5))
+        for xb in range(4):
+            for pair in range(2):
+                add(xb, pair, work(p, xb, pair))
+        for c in range(2):
+            build(p + 1, c, range(4))
+            build(late, c, range(4))
+        return 0
+
+    def sweep(xb, i):
+        p = 16 + 4 * i
+        for pair in range(2):
+            add(xb, pair, sum(work(p + k, xb, pair) for k in range(4)))
+
     def phase_b1(i, _):
-        p = 16 + 2 * i
-
-        @pl.when(i < 7)
+        @pl.when(i < 3)
         def _():
-            w.got_partner(p + 2)
-            w.got_partner(p + 3)
-
-        for pair in range(2):
-            add(3, pair, work(p, 3, pair) + work(p + 1, 3, pair))
-        for k in range(2):
+            for k in range(4):
+                w.got_partner(20 + 4 * i + k)
+
+        sweep(3, i)
+        for k in range(4):
             for c in range(2):
-                build(16 + lax.rem(2 * i + 2 + k, 16), c, range(4))
+                build(16 + lax.rem(4 * i + 4 + k, 16), c, range(4))
         return 0
 
-    def ysend(label, d, slot):
-        return lambda: pltpu.make_async_remote_copy(src_ref=yt.at[label], dst_ref=yin.at[slot], send_sem=xsem.at[4 + slot],
-                                                    recv_sem=xsem.at[7 + slot], device_id=xdev(d), device_id_type=MESH)
-
-    sends = [ysend(3, 2, 2), ysend(2, 1, 0), ysend(1, -1, 1)]
+    def ysend(label, d, slot, pair):
+        tiles = pl.ds(2 * pair, 2)
+        return lambda: pltpu.make_async_remote_copy(
+            src_ref=yt.at[label, tiles], dst_ref=yin.at[slot, tiles], send_sem=ysem.at[0, slot, pair],
+            recv_sem=ysem.at[1, slot, pair], device_id=xdev(d), device_id_type=MESH)
+
+    sends = [[ysend(*who, pair) for pair in range(2)] for who in ((3, 2, 2), (2, 1, 0), (1, -1, 1))]
 
     def phase_b2(i, _):
         for n in range(3):
-            pl.when(i == 8 * n + 1)(lambda n=n: sends[n]().start())
-        xb, p = 2 - lax.div(i, 8), 16 + 2 * lax.rem(i, 8)
-        for pair in range(2):
-            add(xb, pair, work(p, xb, pair) + work(p + 1, xb, pair))
+            for pair in range(2):
+                pl.when(i == 4 * n + pair)(lambda n=n, pair=pair: sends[n][pair]().start())
+        sweep(2 - lax.div(i, 4), lax.rem(i, 4))
         return 0
 
     for p in range(2):
@@ -278,14 +296,13 @@
     xgot(2, (0, 4), 1)
     xcopy(1, 3, (0, 2), 2, 1)
     xcopy(2, 3, (2, 2), 3, -1)
-    lax.fori_loop(0, 32, phase_a, 0)
-    w.got_partner(17)
-    for c in range(2):
-        build(17, c, range(4))
-    lax.fori_loop(0, 8, phase_b1, 0)
-    lax.fori_loop(0, 24, phase_b2, 0)
-    for cp in sends:
-        cp().wait()
+    lax.fori_loop(0, 4, phase_a, 0)
+    lax.fori_loop(0, 14, phase_a4, 0)
+    lax.fori_loop(0, 4, phase_b1, 0)
+    lax.fori_loop(0, 12, phase_b2, 0)
+    for pairs in sends:
+        for cp in pairs:
+            cp().wait()
     for wait in w.sent:
         wait()
     for t in range(4):
@@ -332,7 +349,8 @@
                 pltpu.SemaphoreType.DMA((100,)),
                 pltpu.SemaphoreType.DMA((NPOS, 2)),
                 pltpu.SemaphoreType.DMA((NPOS,)),
-                pltpu.SemaphoreType.DMA((10,)),
+                pltpu.SemaphoreType.DMA((4,)),
+                pltpu.SemaphoreType.DMA((2, 3, 2)),
             ],
             compiler_params=pltpu.CompilerParams(vmem_limit_bytes=60 * 2 ** 20, collective_id=0, has_side_effects=True),
         )(scal, own, xown)

time: 155 us -> 152 us (0.981)
  Pallas kernels: 147 us -> 144 us
    pallas_call x1, Pallas kernels: 147 us -> 144 us  [per_device(): pl.pallas_call(kernel, out_shape=jax.ShapeDtypeStruct((BLK, 128), F32), n...]
where the time goes in v3:
time: 152 us
  Pallas kernels  144 us (95%)
  local copies, waits for them, and re-layouts  3.26 us (2%)
  other arithmetic  2.43 us (2%)
  between operations  1.57 us (1%)
    pallas_call x1, Pallas kernels, per_device(): pl.pallas_call(kernel, out_shape=jax.ShapeDtypeStruct((BLK, 128), F32), n...  144 us

profile of v3, /device:TPU:1, one launch (start us, length us, event | category | flops | bytes accessed | tf_op | source)
XLA Modules:
  0.0 151.6 jit_solution(11722760269942192295)
XLA Ops:
  0.0 0.0 copy-start
  1.5 0.6 pad_maximum_fusion.2.scal_ref
  2.1 1.1 copy.6
  3.2 0.0 copy-done
  3.2 0.2 fusion.1
  3.4 0.2 copy.7
  3.8 0.7 pad_maximum_fusion.1.xown_ref
  4.6 0.8 pad_maximum_fusion.own_ref
  5.4 144.3 %comm.1 = f32[1024,128]{1,0:T(8,128)} custom-call(f32[4]{0:T(128)} %pad_maximum_fusion.2.scal_ref, bf16[2,1056,128]{2,1,0:T(8,128)(2,1)} %pad_maximum_fusion.own_ref, bf16[4,2,144,128]{3,2,1,0:T(8,128)(2,1)} %pad_maximum_fusion.1.xown_ref), custom_call_target="tpu_custom_call" | custom-call | tf_op jit(solution)/shard_map/comm/pallas_call | solution.py:336
  149.7 1.9 %copy.14 = f32[1024,128]{1,0:T(8,128)} copy(f32[1024,128]{1,0:T(8,128)} %comm.1) | data formatting | bytes 1048576
  (9 shorter events, 0.1 us)
Async XLA Ops:
  0.0 3.2 %copy-start = (bf16[1024,128]{1,0:T(8,128)(2,1)S(1)}, bf16[1024,128]{1,0:T(8,128)(2,1)}, u32[]{:S(2)}) copy-start(bf16[1024,128]{1,0:T(8,128)(2,1)} %param.4) | copy-start | bytes 786436

commit v4 on v3

--- a/solution.py
+++ b/solution.py
@@ -37,10 +37,10 @@
 
 
 def split3(n):
-    hi = lax.reduce_precision(jnp.minimum(n, BF16_MAX), 8, 7)
+    hi = jnp.minimum(n, BF16_MAX).astype(BF16).astype(F32)
     r = n - hi
-    mid = lax.reduce_precision(r, 8, 7)
-    return hi.astype(BF16), mid.astype(BF16), (r - mid).astype(BF16)
+    mid = r.astype(BF16).astype(F32)
+    return hi, mid, r - mid
 
 
 class Wires:
@@ -158,13 +158,13 @@
     return {1: slot1, 4: slot2, 8: slot3, 9: slot4, 10: slot5, 12: slot6, 14: slot7, 15: slot8}
 
 
-def kernel(scal_ref, own_ref, xown_ref, out_ref, cols, ag, xr, yt, yin, local, send, ici, d2d, xsem, ysem):
+def kernel(ell_ref, scale_ref, x_ref, v_ref, out_ref, cols, ag, xr, yt, yin, vbuf, local, send, ici, d2d, xsem, ysem):
     pos = {k: lax.axis_index(k) for k in ('c', 'z', 'y', 'x')}
     w = Wires(cols, send, ici, d2d, pos)
     xdev = lambda d: w.dev['x', d]
 
-    loads = [pltpu.make_async_copy(own_ref.at[h], cols.at[h, 0], local.at[h]) for h in range(2)]
-    loads.append(pltpu.make_async_copy(xown_ref, xr.at[0, :, :, pl.ds(0, XROWS)], local.at[2]))
+    loads = [pltpu.make_async_copy(x_ref.at[pl.ds(h * HALF, HALF)], cols.at[h, 0, pl.ds(0, HALF)], local.at[h]) for h in range(2)]
+    loads.append(pltpu.make_async_copy(v_ref, vbuf, local.at[2]))
     for cp in loads:
         cp.start()
     barrier = pltpu.get_barrier_semaphore()
@@ -173,8 +173,30 @@
         pl.semaphore_signal(barrier, inc=1, device_id=dev, device_id_type=MESH)
     xr[:, :, :, pl.ds(XROWS, TILE - XROWS), :] = jnp.zeros((4, 4, 2, TILE - XROWS, 128), BF16)
     yt[...] = jnp.zeros_like(yt)
+
+    ell = jnp.full((8, 128), ell_ref[0], F32)
+    size = jnp.abs(jnp.full((8, 128), scale_ref[0], F32))
+    two_ell_sq = 2.0 * ell * ell
+    shrink = jnp.where(two_ell_sq > 1.0, 2.0 ** -6, 1.0)
+    negc = (-(1.4426950408889634 / shrink) / two_ell_sq)[0, 0]
+    logs = jnp.log2(size)[0, 0]
+    cap = size[0, 0]
+    shrink = shrink[0, 0]
+
     for cp in loads:
         cp.wait()
+    for t in range(8):
+        half, at = t // 4, (t % 4) * 128
+        xt = cols[half, 0, pl.ds(at, 128), :].astype(F32).T
+        hi, mid, lo = split3(jnp.sum(xt * xt, axis=0, keepdims=True))
+        row = lax.broadcasted_iota(jnp.int32, (16, 128), 0)
+        ones = jnp.where(row < 6, 1.0, 0.0)
+        left = jnp.where(row == 0, hi, jnp.where(row == 1, mid, jnp.where(row == 2, lo, ones)))
+        right = jnp.where(row == 3, hi, jnp.where(row == 4, mid, jnp.where(row == 5, lo, ones)))
+        cols[half, 0, pl.ds(AUG0 + (t % 4) * 8, 8), :] = left[:8].astype(BF16)
+        xr[0, t // 2, t % 2, pl.ds(0, 128), :] = (xt * (-2.0 * shrink)).astype(BF16)
+        xr[0, t // 2, t % 2, pl.ds(128, 16), :] = (right * shrink).astype(BF16)
+        cols[half, 0, pl.ds(HALF + at, 128), :] = vbuf[pl.ds(t * 128, 128), :].astype(F32).T.astype(BF16)
     pl.semaphore_wait(barrier, len(peers))
 
     def xcopy(src, dst, tiles, recv, d):
@@ -187,14 +209,13 @@
 
     w.partner((0, 0, A))
     w.partner((0, 0, B))
-    xcopy(0, 1, (0, 4), 0, 1)
-    xcopy(0, 2, (0, 4), 1, -1)
+    for part in range(2):
+        xcopy(0, 1, (2 * part, 2), part, 1)
+        xcopy(0, 2, (2 * part, 2), 2 + part, -1)
     w.both('y', (0, 0, A))
     w.both('z', (0, 0, B))
     w.both('y', (0, 0, B))
     w.both('z', (0, 0, A))
-
-    negc, logs = scal_ref[0], scal_ref[1]
 
     def build(p, c, tiles):
         for lt in tiles:
@@ -207,7 +228,7 @@
         rhs = jnp.concatenate([jnp.concatenate([xr[xb, pair * 2 + q, h] for h in range(2)], axis=1) for q in range(2)], axis=1)
         dist = jnp.dot(lhs, rhs, preferred_element_type=F32)
         kern = jnp.exp2(dist * negc + logs).astype(BF16)
-        kern = jnp.minimum(kern, jnp.full(kern.shape, scal_ref[2], F32).astype(BF16))
+        kern = jnp.minimum(kern, jnp.full(kern.shape, cap, F32).astype(BF16))
         vt = jnp.concatenate([cols[p, c, pl.ds(HALF + 128 * k, 128), :] for c in range(2) for k in range(4)], axis=1)
         return jnp.dot(vt, kern, preferred_element_type=F32)
 
@@ -217,26 +238,43 @@
 
     acts = schedule(w)
 
-    def phase_a(i, _):
-        p, h = lax.div(i, 2), lax.rem(i, 2)
-
-        @pl.when(h == 0)
-        def _():
-                pl.when(p == 1)(acts[1])
-
-        @pl.when(i == 1)
-        def _():
-            xgot(3, (0, 2), 2)
-            xgot(3, (2, 2), 3)
-
-        @pl.when((h == 1) & (p > 0))
-        def _():
-            w.got_partner(p + 1)
-
-        for k in range(2):
-            for pair in range(2):
-                add(2 * h + k, pair, work(p, 2 * h + k, pair))
-        build(p + 1, h, range(4))
+    def phase_0(k, _):
+        @pl.when(k == 2)
+        def _():
+            xgot(1, (0, 2), 0)
+
+        @pl.when(k == 3)
+        def _():
+            xgot(2, (0, 2), 2)
+            xcopy(1, 3, (0, 2), 4, 1)
+
+        @pl.when(k == 4)
+        def _():
+            xgot(1, (2, 2), 1)
+
+        @pl.when(k == 5)
+        def _():
+            xgot(2, (2, 2), 3)
+            xcopy(2, 3, (2, 2), 5, -1)
+            acts[1]()
+
+        @pl.when(k == 6)
+        def _():
+            xgot(3, (0, 2), 4)
+
+        @pl.when(k == 7)
+        def _():
+            xgot(3, (2, 2), 5)
+            w.got_partner(2)
+
+        a, b = lax.div(k, 2), lax.rem(k, 2)
+        e = lax.div(a + 1, 2)
+        inner = lax.rem(e, 2)
+        xb = inner * (1 + b) + (1 - inner) * 3 * lax.div(e, 2)
+        pair = inner * (a - 1) + (1 - inner) * b
+        add(xb, pair, work(0, xb, pair) + work(1, xb, pair))
+        for c in range(2):
+            build(1 + lax.div(k, 7), c, range(4))
         return 0
 
     def phase_a4(n, _):
@@ -289,14 +327,9 @@
 
     for p in range(2):
         w.got_partner(p)
-        if p == 0:
-            for c in range(2):
-                build(p, c, range(4))
-    xgot(1, (0, 4), 0)
-    xgot(2, (0, 4), 1)
-    xcopy(1, 3, (0, 2), 2, 1)
-    xcopy(2, 3, (2, 2), 3, -1)
-    lax.fori_loop(0, 4, phase_a, 0)
+        for c in range(2):
+            build(p, c, range(4))
+    lax.fori_loop(0, 8, phase_0, 0)
     lax.fori_loop(0, 14, phase_a4, 0)
     lax.fori_loop(0, 4, phase_b1, 0)
     lax.fori_loop(0, 12, phase_b2, 0)
@@ -306,8 +339,7 @@
     for wait in w.sent:
         wait()
     for t in range(4):
-        total = (yt[0, t] + yin[0, t] + yin[1, t] + yin[2, t]) * scal_ref[3]
-        out_ref[pl.ds(t * TILE, TILE), :] = total.T
+        out_ref[t] = yt[0, t] + yin[0, t] + yin[1, t] + yin[2, t]
 
 
 def solution(mesh):
@@ -315,29 +347,12 @@
     spec = P(('z', 'y', 'x', 'c'), None)
 
     def per_device(x, v, ell, scale):
-        two_ell_sq = 2.0 * ell[0] * ell[0]
-        s = scale[0]
-        shrink = jnp.where(two_ell_sq > 1.0, 2.0 ** -6, 1.0).astype(F32)
-        negc = -(1.4426950408889634 / shrink) / two_ell_sq
-        scal = jnp.stack([negc, jnp.log2(jnp.abs(s)), jnp.abs(s), jnp.where(s < 0, -1.0, 1.0)])
-
-        norm = jnp.sum(jnp.square(x.astype(F32)), axis=1)
-        pieces = jnp.stack(split3(norm) + (jnp.ones_like(norm, BF16),) * 3)
-        lanes = jnp.pad(pieces, ((0, 2), (0, 0))).reshape(8, 8, 128).transpose(1, 0, 2)
-        vt = v.reshape(8, 128, 128).transpose(0, 2, 1)
-        own = jnp.concatenate([x.reshape(2, HALF, 128), vt.reshape(2, HALF, 128), lanes.reshape(2, 32, 128)], axis=1)
-
-        xt = x.reshape(4, 2, 128, 128).transpose(0, 1, 3, 2).astype(F32) * (-2.0 * shrink)
-        rowpc = jnp.pad(jnp.concatenate([pieces[3:], pieces[:3]]).astype(F32) * shrink, ((0, 10), (0, 0)))
-        rowpc = rowpc.reshape(16, 4, 2, 128).transpose(1, 2, 0, 3)
-        xown = jnp.concatenate([xt, rowpc], axis=2).astype(BF16)
-
-        anym = pl.BlockSpec(memory_space=pl.ANY)
-        return pl.pallas_call(
+        anym, smem = pl.BlockSpec(memory_space=pl.ANY), pl.BlockSpec(memory_space=pltpu.SMEM)
+        yt = pl.pallas_call(
             kernel,
-            out_shape=jax.ShapeDtypeStruct((BLK, 128), F32),
+            out_shape=jax.ShapeDtypeStruct((4, 128, TILE), F32),
             name='comm',
-            in_specs=[pl.BlockSpec(memory_space=pltpu.SMEM), anym, anym],
+            in_specs=[smem, smem, anym, anym],
             out_specs=pl.BlockSpec(memory_space=pltpu.VMEM),
             scratch_shapes=[
                 pltpu.VMEM((NPOS, 2, ROWS, 128), BF16),
@@ -345,14 +360,16 @@
                 pltpu.VMEM((4, 4, 2, TILE, 128), BF16),
                 pltpu.VMEM((4, 4, 128, TILE), F32),
                 pltpu.VMEM((3, 4, 128, TILE), F32),
+                pltpu.VMEM((BLK, 128), BF16),
                 pltpu.SemaphoreType.DMA((3,)),
                 pltpu.SemaphoreType.DMA((100,)),
                 pltpu.SemaphoreType.DMA((NPOS, 2)),
                 pltpu.SemaphoreType.DMA((NPOS,)),
-                pltpu.SemaphoreType.DMA((4,)),
+                pltpu.SemaphoreType.DMA((6,)),
                 pltpu.SemaphoreType.DMA((2, 3, 2)),
             ],
             compiler_params=pltpu.CompilerParams(vmem_limit_bytes=60 * 2 ** 20, collective_id=0, has_side_effects=True),
-        )(scal, own, xown)
+        )(ell, scale, x, v)
+        return yt.transpose(0, 2, 1).reshape(BLK, 128) * jnp.where(scale[0] < 0, -1.0, 1.0)
 
     return jax.shard_map(per_device, mesh=grid, in_specs=(spec, spec, P(None), P(None)), out_specs=spec, check_vma=False)

time: 152 us -> 143 us (0.941)
  Pallas kernels: 144 us -> 138 us
  local copies, waits for them, and re-layouts: 3.26 us -> 1 us
    pallas_call x1, Pallas kernels: 144 us -> 138 us  [per_device(): pl.pallas_call(kernel, out_shape=jax.ShapeDtypeStruct((4, 128, TILE), F32...]
    unnamed x3 -> x0, local copies, waits for them, and re-layouts: 1.87 us -> none
    concatenate x2 -> x0, other arithmetic: 1.55 us -> none  [the longest x1 0.82 us: per_device(): jnp.concatenate([x.reshape(2, HALF, 128), vt.reshape(2, HALF, 128), lanes...]
where the time goes in v4:
time: 143 us; the launch traced here: 142 us
  Pallas kernels  138 us (97%)
    pallas_call x1, Pallas kernels, per_device(): pl.pallas_call(kernel, out_shape=jax.ShapeDtypeStruct((4, 128, TILE), F32...  138 us

profile of v4, /device:TPU:1, one launch (start us, length us, event | category | flops | bytes accessed | tf_op | source)
XLA Modules:
  0.0 141.6 jit_solution(868501215499197943)
XLA Ops:
  1.3 138.2 %comm.1 = f32[4,128,256]{2,1,0:T(8,128)} custom-call(f32[1]{0:T(128)S(6)} %copy.6.ell_ref, f32[1]{0:T(128)S(6)} %copy.7.scale_ref, bf16[1024,128]{1,0:T(8,128)(2,1)} %x_ref.1, bf16[1024,128]{1,0:T(8,128)(2,1)} %v_ref.1), custom_call_target="tpu_custom_call" | custom-call | tf_op jit(solution)/shard_map/comm/pallas_call | solution.py:351
  139.5 1.1 multiply_bitcast_fusion
  140.6 1.0 copy.5

commit v5 on v4

--- a/solution.py
+++ b/solution.py
@@ -17,6 +17,8 @@
 ROWS = AUG0 + 4 * 8
 XROWS = 144
 BF16_MAX = 3.3895313892515355e38
+CORES = ((0,), (1,))
+AHEAD = True
 
 A, B = 0, 1
 ORDER = [(0, 0, A), (0, 0, B),
@@ -177,25 +179,28 @@
     ell = jnp.full((8, 128), ell_ref[0], F32)
     size = jnp.abs(jnp.full((8, 128), scale_ref[0], F32))
     two_ell_sq = 2.0 * ell * ell
-    shrink = jnp.where(two_ell_sq > 1.0, 2.0 ** -6, 1.0)
-    negc = (-(1.4426950408889634 / shrink) / two_ell_sq)[0, 0]
-    logs = jnp.log2(size)[0, 0]
-    cap = size[0, 0]
-    shrink = shrink[0, 0]
+    unit = jnp.exp2(jnp.clip(-jnp.ceil(jnp.log2(two_ell_sq)), -126.0, 40.0)).astype(BF16).astype(F32)
+    unit = jnp.where(two_ell_sq > 3.4028234e38, 0.0, unit)
+    factor = jnp.where(unit > 0.0, -1.4426950408889634 / (unit * two_ell_sq), -1.0)
+    shift = jnp.maximum(jnp.log2(size), -400.0) / factor
+    negc, cap = factor[0, 0], size[0, 0]
+    unit, shift = unit[:1], shift[:1]
 
     for cp in loads:
         cp.wait()
     for t in range(8):
         half, at = t // 4, (t % 4) * 128
         xt = cols[half, 0, pl.ds(at, 128), :].astype(F32).T
-        hi, mid, lo = split3(jnp.sum(xt * xt, axis=0, keepdims=True))
+        norm = jnp.sum(xt * xt, axis=0, keepdims=True)
+        hi, mid, lo = split3(norm)
         row = lax.broadcasted_iota(jnp.int32, (16, 128), 0)
         ones = jnp.where(row < 6, 1.0, 0.0)
         left = jnp.where(row == 0, hi, jnp.where(row == 1, mid, jnp.where(row == 2, lo, ones)))
-        right = jnp.where(row == 3, hi, jnp.where(row == 4, mid, jnp.where(row == 5, lo, ones)))
+        hi, mid, lo = split3(norm * unit + shift)
+        right = jnp.where(row == 3, hi, jnp.where(row == 4, mid, jnp.where(row == 5, lo, ones * unit)))
         cols[half, 0, pl.ds(AUG0 + (t % 4) * 8, 8), :] = left[:8].astype(BF16)
-        xr[0, t // 2, t % 2, pl.ds(0, 128), :] = (xt * (-2.0 * shrink)).astype(BF16)
-        xr[0, t // 2, t % 2, pl.ds(128, 16), :] = (right * shrink).astype(BF16)
+        xr[0, t // 2, t % 2, pl.ds(0, 128), :] = (xt * (-2.0 * unit)).astype(BF16)
+        xr[0, t // 2, t % 2, pl.ds(128, 16), :] = right.astype(BF16)
         cols[half, 0, pl.ds(HALF + at, 128), :] = vbuf[pl.ds(t * 128, 128), :].astype(F32).T.astype(BF16)
     pl.semaphore_wait(barrier, len(peers))
 
@@ -223,18 +228,32 @@
             full = jnp.concatenate([piece, jnp.zeros((120, 128), F32)], axis=0)
             ag[p, c, pl.ds(lt * 128, 128), :] = full.T.astype(BF16)
 
-    def work(p, xb, pair):
-        lhs = jnp.concatenate([jnp.concatenate([cols[p, c, pl.ds(0, HALF), :], ag[p, c]], axis=1) for c in range(2)], axis=0)
+    def gram(p, xb, pair, cores):
+        lhs = jnp.concatenate([jnp.concatenate([cols[p, c, pl.ds(0, HALF), :], ag[p, c]], axis=1) for c in cores], axis=0)
         rhs = jnp.concatenate([jnp.concatenate([xr[xb, pair * 2 + q, h] for h in range(2)], axis=1) for q in range(2)], axis=1)
-        dist = jnp.dot(lhs, rhs, preferred_element_type=F32)
-        kern = jnp.exp2(dist * negc + logs).astype(BF16)
+        return jnp.dot(lhs, rhs, preferred_element_type=F32)
+
+    def apply(p, dist, cores):
+        kern = jnp.exp2(dist * negc).astype(BF16)
         kern = jnp.minimum(kern, jnp.full(kern.shape, cap, F32).astype(BF16))
-        vt = jnp.concatenate([cols[p, c, pl.ds(HALF + 128 * k, 128), :] for c in range(2) for k in range(4)], axis=1)
+        vt = jnp.concatenate([cols[p, c, pl.ds(HALF + 128 * k, 128), :] for c in cores for k in range(4)], axis=1)
         return jnp.dot(vt, kern, preferred_element_type=F32)
 
-    def add(xb, pair, r):
-        for q in range(2):
-            yt[xb, pair * 2 + q] += r[:, q * TILE:(q + 1) * TILE]
+    def group(work):
+        todo = [(p, xb, pair, cores, i) for i, (ps, xb, pair) in enumerate(work) for p in ps for cores in CORES]
+        sums = [None] * len(work)
+        dist = gram(*todo[0][:4])
+        for n, (p, xb, pair, cores, i) in enumerate(todo):
+            now = dist
+            if n + 1 < len(todo) and AHEAD:
+                dist = gram(*todo[n + 1][:4])
+            r = apply(p, now, cores)
+            if n + 1 < len(todo) and not AHEAD:
+                dist = gram(*todo[n + 1][:4])
+            sums[i] = r if sums[i] is None else sums[i] + r
+            if n + 1 == len(todo) or todo[n + 1][4] != i:
+                for q in range(2):
+                    yt[xb, pair * 2 + q] += sums[i][:, q * TILE:(q + 1) * TILE]
 
     acts = schedule(w)
 
@@ -272,7 +291,7 @@
         inner = lax.rem(e, 2)
         xb = inner * (1 + b) + (1 - inner) * 3 * lax.div(e, 2)
         pair = inner * (a - 1) + (1 - inner) * b
-        add(xb, pair, work(0, xb, pair) + work(1, xb, pair))
+        group([((0, 1), xb, pair)])
         for c in range(2):
             build(1 + lax.div(k, 7), c, range(4))
         return 0
@@ -285,9 +304,7 @@
         w.got_partner(p + 1)
         late = p + lax.div(p, 12) * (5 - 3 * lax.div(p, 15))
         pl.when((p >= 12) & (p < 15))(lambda: w.got_partner(p + 5))
-        for xb in range(4):
-            for pair in range(2):
-                add(xb, pair, work(p, xb, pair))
+        group([((p,), xb, pair) for xb in range(4) for pair in range(2)])
         for c in range(2):
             build(p + 1, c, range(4))
             build(late, c, range(4))
@@ -295,8 +312,7 @@
 
     def sweep(xb, i):
         p = 16 + 4 * i
-        for pair in range(2):
-            add(xb, pair, sum(work(p + k, xb, pair) for k in range(4)))
+        group([([p + k for k in range(4)], xb, pair) for pair in range(2)])
 
     def phase_b1(i, _):
         @pl.when(i < 3)

time: 143 us -> 140 us (0.979)
  Pallas kernels: 138 us -> 136 us
    pallas_call x1, Pallas kernels: 138 us -> 136 us  [per_device(): pl.pallas_call(kernel, out_shape=jax.ShapeDtypeStruct((4, 128, TILE), F32...]
where the time goes in v5:
time: 140 us; the launch traced here: 139 us
  Pallas kernels  136 us (97%)
    pallas_call x1, Pallas kernels, per_device(): pl.pallas_call(kernel, out_shape=jax.ShapeDtypeStruct((4, 128, TILE), F32...  136 us

profile of v5, /device:TPU:1, one launch (start us, length us, event | category | flops | bytes accessed | tf_op | source)
XLA Modules:
  0.0 139.0 jit_solution(7299887108441459282)
XLA Ops:
  1.3 135.6 %comm.1 = f32[4,128,256]{2,1,0:T(8,128)} custom-call(f32[1]{0:T(128)S(6)} %copy.6.ell_ref, f32[1]{0:T(128)S(6)} %copy.7.scale_ref, bf16[1024,128]{1,0:T(8,128)(2,1)} %x_ref.1, bf16[1024,128]{1,0:T(8,128)(2,1)} %v_ref.1), custom_call_target="tpu_custom_call" | custom-call | tf_op jit(solution)/shard_map/comm/pallas_call | solution.py:367
  136.9 1.1 multiply_bitcast_fusion
  138.0 1.0 copy.5

commit v6 on v5

--- a/solution.py
+++ b/solution.py
@@ -184,6 +184,7 @@
     factor = jnp.where(unit > 0.0, -1.4426950408889634 / (unit * two_ell_sq), -1.0)
     shift = jnp.maximum(jnp.log2(size), -400.0) / factor
     negc, cap = factor[0, 0], size[0, 0]
+    sign = jnp.where(jnp.full((8, 128), scale_ref[0], F32) < 0.0, -1.0, 1.0)[0, 0]
     unit, shift = unit[:1], shift[:1]
 
     for cp in loads:
@@ -270,34 +271,40 @@
         @pl.when(k == 4)
         def _():
             xgot(1, (2, 2), 1)
-
-        @pl.when(k == 5)
-        def _():
             xgot(2, (2, 2), 3)
             xcopy(2, 3, (2, 2), 5, -1)
+
+        @pl.when(k == 5)
+        def _():
             acts[1]()
 
         @pl.when(k == 6)
         def _():
+            for p in (2, 3):
+                w.got_partner(p)
+                for c in range(2):
+                    build(p, c, range(4))
+
+        @pl.when(k == 7)
+        def _():
+            w.got_partner(4)
+
+        p, n = 2 * lax.div(k, 6), lax.rem(k, 6)
+        a, b = lax.div(n, 2), lax.rem(n, 2)
+        inner = lax.div(a + 1, 2)
+        group([((p, p + 1), inner * (1 + b), inner * (a - 1) + (1 - inner) * b)])
+        for c in range(2):
+            build(1 + 3 * lax.div(k, 7), c, range(4))
+        return 0
+
+    def phase_a4(n, _):
+        p = n + 4
+
+        @pl.when(p == 4)
+        def _():
             xgot(3, (0, 2), 4)
-
-        @pl.when(k == 7)
-        def _():
             xgot(3, (2, 2), 5)
-            w.got_partner(2)
-
-        a, b = lax.div(k, 2), lax.rem(k, 2)
-        e = lax.div(a + 1, 2)
-        inner = lax.rem(e, 2)
-        xb = inner * (1 + b) + (1 - inner) * 3 * lax.div(e, 2)
-        pair = inner * (a - 1) + (1 - inner) * b
-        group([((0, 1), xb, pair)])
-        for c in range(2):
-            build(1 + lax.div(k, 7), c, range(4))
-        return 0
-
-    def phase_a4(n, _):
-        p = n + 2
+
         for at, act in acts.items():
             if at > 1:
                 pl.when(p == at)(act)
@@ -311,7 +318,7 @@
         return 0
 
     def sweep(xb, i):
-        p = 16 + 4 * i
+        p = lax.rem(16 + 4 * i, 32)
         group([([p + k for k in range(4)], xb, pair) for pair in range(2)])
 
     def phase_b1(i, _):
@@ -345,9 +352,9 @@
         w.got_partner(p)
         for c in range(2):
             build(p, c, range(4))
-    lax.fori_loop(0, 8, phase_0, 0)
-    lax.fori_loop(0, 14, phase_a4, 0)
-    lax.fori_loop(0, 4, phase_b1, 0)
+    lax.fori_loop(0, 12, phase_0, 0)
+    lax.fori_loop(0, 12, phase_a4, 0)
+    lax.fori_loop(0, 5, phase_b1, 0)
     lax.fori_loop(0, 12, phase_b2, 0)
     for pairs in sends:
         for cp in pairs:
@@ -355,7 +362,7 @@
     for wait in w.sent:
         wait()
     for t in range(4):
-        out_ref[t] = yt[0, t] + yin[0, t] + yin[1, t] + yin[2, t]
+        out_ref[t] = (yt[0, t] + yin[0, t] + yin[1, t] + yin[2, t]) * sign
 
 
 def solution(mesh):
@@ -386,6 +393,6 @@
             ],
             compiler_params=pltpu.CompilerParams(vmem_limit_bytes=60 * 2 ** 20, collective_id=0, has_side_effects=True),
         )(ell, scale, x, v)
-        return yt.transpose(0, 2, 1).reshape(BLK, 128) * jnp.where(scale[0] < 0, -1.0, 1.0)
+        return yt.transpose(0, 2, 1).reshape(BLK, 128)
 
     return jax.shard_map(per_device, mesh=grid, in_specs=(spec, spec, P(None), P(None)), out_specs=spec, check_vma=False)

time: 140 us -> 141 us (level)
  Pallas kernels: 136 us -> 138 us
    pallas_call x1, Pallas kernels: 136 us -> 138 us  [per_device(): pl.pallas_call(kernel, out_shape=jax.ShapeDtypeStruct((4, 128, TILE), F32...]
    transpose x0 -> x1, local copies, waits for them, and re-layouts: none -> 2.04 us  [per_device(): return yt.transpose(0, 2, 1).reshape(BLK, 128)]
where the time goes in v6:
time: 141 us
  Pallas kernels  138 us (98%)
  local copies, waits for them, and re-layouts  2.04 us (1%)
    pallas_call x1, Pallas kernels, per_device(): pl.pallas_call(kernel, out_shape=jax.ShapeDtypeStruct((4, 128, TILE), F32...  138 us

profile of v6, /device:TPU:1, one launch (start us, length us, event | category | flops | bytes accessed | tf_op | source)
XLA Modules:
  0.0 141.0 jit_solution(13492569333471952928)
XLA Ops:
  1.3 137.7 %comm.1 = f32[4,128,256]{2,1,0:T(8,128)} custom-call(f32[1]{0:T(128)S(6)} %copy.6.ell_ref, f32[1]{0:T(128)S(6)} %copy.7.scale_ref, bf16[1024,128]{1,0:T(8,128)(2,1)} %x_ref.1, bf16[1024,128]{1,0:T(8,128)(2,1)} %v_ref.1), custom_call_target="tpu_custom_call" | custom-call | tf_op jit(solution)/shard_map/comm/pallas_call | solution.py:374
  139.0 2.0 %copy.5 = f32[4,256,128]{2,1,0:T(8,128)} copy(f32[4,256,128]{1,2,0:T(8,128)} %bitcast.2) | data formatting | bytes 1048576 | tf_op jit(solution)/shard_map/transpose | solution.py:396

commit v7 on v5

--- a/solution.py
+++ b/solution.py
@@ -17,8 +17,6 @@
 ROWS = AUG0 + 4 * 8
 XROWS = 144
 BF16_MAX = 3.3895313892515355e38
-CORES = ((0,), (1,))
-AHEAD = True
 
 A, B = 0, 1
 ORDER = [(0, 0, A), (0, 0, B),
@@ -184,6 +182,7 @@
     factor = jnp.where(unit > 0.0, -1.4426950408889634 / (unit * two_ell_sq), -1.0)
     shift = jnp.maximum(jnp.log2(size), -400.0) / factor
     negc, cap = factor[0, 0], size[0, 0]
+    sign = jnp.where(jnp.full((8, 128), scale_ref[0], F32) < 0.0, -1.0, 1.0)[0, 0]
     unit, shift = unit[:1], shift[:1]
 
     for cp in loads:
@@ -233,27 +232,24 @@
         rhs = jnp.concatenate([jnp.concatenate([xr[xb, pair * 2 + q, h] for h in range(2)], axis=1) for q in range(2)], axis=1)
         return jnp.dot(lhs, rhs, preferred_element_type=F32)
 
-    def apply(p, dist, cores):
+    def values(dist):
         kern = jnp.exp2(dist * negc).astype(BF16)
-        kern = jnp.minimum(kern, jnp.full(kern.shape, cap, F32).astype(BF16))
+        return jnp.minimum(kern, jnp.full(kern.shape, cap, F32).astype(BF16))
+
+    def product(p, xb, pair, cores, kern):
         vt = jnp.concatenate([cols[p, c, pl.ds(HALF + 128 * k, 128), :] for c in cores for k in range(4)], axis=1)
-        return jnp.dot(vt, kern, preferred_element_type=F32)
+        r = jnp.dot(vt, kern, preferred_element_type=F32)
+        for q in range(2):
+            yt[xb, pair * 2 + q] += r[:, q * TILE:(q + 1) * TILE]
 
     def group(work):
-        todo = [(p, xb, pair, cores, i) for i, (ps, xb, pair) in enumerate(work) for p in ps for cores in CORES]
-        sums = [None] * len(work)
-        dist = gram(*todo[0][:4])
-        for n, (p, xb, pair, cores, i) in enumerate(todo):
+        todo = [(p, xb, pair, cores) for ps, xb, pair in work for p in ps for cores in ((0,), (1,))]
+        dist = gram(*todo[0])
+        for n, (p, xb, pair, cores) in enumerate(todo):
             now = dist
-            if n + 1 < len(todo) and AHEAD:
-                dist = gram(*todo[n + 1][:4])
-            r = apply(p, now, cores)
-            if n + 1 < len(todo) and not AHEAD:
-                dist = gram(*todo[n + 1][:4])
-            sums[i] = r if sums[i] is None else sums[i] + r
-            if n + 1 == len(todo) or todo[n + 1][4] != i:
-                for q in range(2):
-                    yt[xb, pair * 2 + q] += sums[i][:, q * TILE:(q + 1) * TILE]
+            if n + 1 < len(todo):
+                dist = gram(*todo[n + 1])
+            product(p, xb, pair, cores, values(now))
 
     acts = schedule(w)
 
@@ -355,7 +351,7 @@
     for wait in w.sent:
         wait()
     for t in range(4):
-        out_ref[t] = yt[0, t] + yin[0, t] + yin[1, t] + yin[2, t]
+        out_ref[t] = (yt[0, t] + yin[0, t] + yin[1, t] + yin[2, t]) * sign
 
 
 def solution(mesh):
@@ -386,6 +382,6 @@
             ],
             compiler_params=pltpu.CompilerParams(vmem_limit_bytes=60 * 2 ** 20, collective_id=0, has_side_effects=True),
         )(ell, scale, x, v)
-        return yt.transpose(0, 2, 1).reshape(BLK, 128) * jnp.where(scale[0] < 0, -1.0, 1.0)
+        return yt.transpose(0, 2, 1).reshape(BLK, 128)
 
     return jax.shard_map(per_device, mesh=grid, in_specs=(spec, spec, P(None), P(None)), out_specs=spec, check_vma=False)

time: 140 us -> 138 us (0.986)
  Pallas kernels: 136 us -> 134 us
    pallas_call x1, Pallas kernels: 136 us -> 134 us  [per_device(): pl.pallas_call(kernel, out_shape=jax.ShapeDtypeStruct((4, 128, TILE), F32...]
    transpose x0 -> x1, local copies, waits for them, and re-layouts: none -> 2.04 us  [per_device(): return yt.transpose(0, 2, 1).reshape(BLK, 128)]
where the time goes in v7:
time: 138 us; the launch traced here: 137 us
  Pallas kernels  134 us (97%)
  local copies, waits for them, and re-layouts  2.04 us (1%)
    pallas_call x1, Pallas kernels, per_device(): pl.pallas_call(kernel, out_shape=jax.ShapeDtypeStruct((4, 128, TILE), F32...  134 us

profile of v7, /device:TPU:1, one launch (start us, length us, event | category | flops | bytes accessed | tf_op | source)
XLA Modules:
  0.0 136.9 jit_solution(20835819849817661)
XLA Ops:
  1.3 133.5 %comm.1 = f32[4,128,256]{2,1,0:T(8,128)} custom-call(f32[1]{0:T(128)S(6)} %copy.6.ell_ref, f32[1]{0:T(128)S(6)} %copy.7.scale_ref, bf16[1024,128]{1,0:T(8,128)(2,1)} %x_ref.1, bf16[1024,128]{1,0:T(8,128)(2,1)} %v_ref.1), custom_call_target="tpu_custom_call" | custom-call | tf_op jit(solution)/shard_map/comm/pallas_call | solution.py:363
  134.8 2.0 %copy.5 = f32[4,256,128]{2,1,0:T(8,128)} copy(f32[4,256,128]{1,2,0:T(8,128)} %bitcast.2) | data formatting | bytes 1048576 | tf_op jit(solution)/shard_map/transpose | solution.py:385

commit v8 on v7

--- a/solution.py
+++ b/solution.py
@@ -333,8 +333,9 @@
     def phase_b2(i, _):
         for n in range(3):
             for pair in range(2):
-                pl.when(i == 4 * n + pair)(lambda n=n, pair=pair: sends[n][pair]().start())
-        sweep(2 - lax.div(i, 4), lax.rem(i, 4))
+                pl.when(i == 2 * n + pair)(lambda n=n, pair=pair: sends[n][pair]().start())
+        p = 16 + 8 * lax.rem(i, 2)
+        group([([p + k for k in range(8)], 2 - lax.div(i, 2), pair) for pair in range(2)])
         return 0
 
     for p in range(2):
@@ -344,7 +345,7 @@
     lax.fori_loop(0, 8, phase_0, 0)
     lax.fori_loop(0, 14, phase_a4, 0)
     lax.fori_loop(0, 4, phase_b1, 0)
-    lax.fori_loop(0, 12, phase_b2, 0)
+    lax.fori_loop(0, 6, phase_b2, 0)
     for pairs in sends:
         for cp in pairs:
             cp().wait()

time: 138 us -> 137 us (level)
  Pallas kernels: 134 us -> 132 us
where the time goes in v8:
time: 137 us; the launch traced here: 136 us
  Pallas kernels  132 us (96%)
  local copies, waits for them, and re-layouts  2.04 us (1%)
    pallas_call x1, Pallas kernels, per_device(): pl.pallas_call(kernel, out_shape=jax.ShapeDtypeStruct((4, 128, TILE), F32...  132 us

profile of v8, /device:TPU:1, one launch (start us, length us, event | category | flops | bytes accessed | tf_op | source)
XLA Modules:
  0.0 135.6 jit_solution(7892470597663544207)
XLA Ops:
  1.3 132.2 %comm.1 = f32[4,128,256]{2,1,0:T(8,128)} custom-call(f32[1]{0:T(128)S(6)} %copy.6.ell_ref, f32[1]{0:T(128)S(6)} %copy.7.scale_ref, bf16[1024,128]{1,0:T(8,128)(2,1)} %x_ref.1, bf16[1024,128]{1,0:T(8,128)(2,1)} %v_ref.1), custom_call_target="tpu_custom_call" | custom-call | tf_op jit(solution)/shard_map/comm/pallas_call | solution.py:364
  133.5 2.0 %copy.5 = f32[4,256,128]{2,1,0:T(8,128)} copy(f32[4,256,128]{1,2,0:T(8,128)} %bitcast.2) | data formatting | bytes 1048576 | tf_op jit(solution)/shard_map/transpose | solution.py:386
